TPU v7x, 32 devices: a whole 2x2x4 slice. The times are simulated.
32 devices in a mesh: win: 2 (over y), dx: 4 (over z), dy: 2 (over x), dz: 2 (over core).
Axes of the slice: x: 2, y: 2, z: 4, core: 2. Of those that a mesh axis runs over, the one named last changes fastest.
Arguments:
- fraction: float32 [3, 8, 2, 2, 768], P(None, ('win', 'dx'), 'dy', 'dz'), parts along dimension 1, may hold values from 0 to 1
- atom_type: int32 [8, 2, 2, 768], P(('win', 'dx'), 'dy', 'dz'), parts along dimension 0, may hold values from 0 to 31
- perturbed: int32 [8, 2, 2, 768], P(('win', 'dx'), 'dy', 'dz'), parts along dimension 0, may hold values from 0 to 1
- leaving: int32 [8, 2, 2, 2, 16], P(('win', 'dx'), 'dy', 'dz'), parts along dimension 0, may hold values from 0 to 767, as said below
- neighbours: int32 [8, 2, 2, 6, 16], P(('win', 'dx'), 'dy', 'dz'), parts along dimension 0, may hold values from 0 to 161, as said below
- counts: int32 [8, 2, 2, 6], P(('win', 'dx'), 'dy', 'dz'), parts along dimension 0, may hold values from 1 to 16, as said below
- sigma_table: float32 [32], replicated, may hold values from 0.8 to 1.2
- depth_table: float32 [32], replicated, may hold values from 0.002 to 0.03
- charge_table: float32 [32], replicated, may hold values from -1 to 1
- domain_edge: float32 [3], replicated, may hold values from 1 to 1.12
- coupling: float32 [2], P('win'), parts along dimension 0, may hold values from 0.1 to 0.9
Outputs:
- forces: float32 [3, 8, 2, 2, 768], P(None, ('win', 'dx'), 'dy', 'dz'), parts along dimension 1
- energy: float32 [2], P('win'), parts along dimension 0
- dhdl: float32 [2], P('win'), parts along dimension 0
There are 2 independent parts, one for each index of `win`. A program takes and returns all parts, laid end to end along the dimension named above; an argument that names none is the same for every part. Nothing has to cross between parts.
Inputs may be any that keep to these rules, and one draw needn't show every extreme that they name: `leaving`: each domain lists 2 * 16 distinct slots: the first 16 leave toward the next domain, the last 16 toward the previous one. `neighbours`: each list holds 16 distinct ghost block numbers; entries at or past the block's count are valid numbers and are not used. `counts`: some block lists exactly 16 blocks in every draw.
All inputs are finite; a program needn't handle non-finite values.
Results may differ from a plain program's by a relative error of at most 0.0003.
Values sent between devices are 32-bit elements; how exact they have to be, the bound alone decides.
A program may use at most 64 MiB of HBM per device.

v0:
```python
import jax
import jax.numpy as jnp
from jax import lax
from jax.sharding import PartitionSpec as P

soft_base = 0.3
soft_alpha = 0.5
charge_base = 0.3
charge_alpha = 0.5
coulomb = 0.1


def passed_along(array, axis, by):
    devices = lax.axis_size(axis)
    return lax.ppermute(array, axis, [(i, (i + by) % devices) for i in range(devices)])


def extended(block, sides, width):
    for axis, dim in sides:
        count = lax.axis_size(axis)
        forward = [(i, i + 1) for i in range(count - 1)]
        forward.append((count - 1, 0))
        backward = [(target, source) for source, target in forward]
        low = lax.ppermute(
            lax.slice_in_dim(block, block.shape[dim] - width, None, axis=dim), axis, forward
        )
        high = lax.ppermute(lax.slice_in_dim(block, 0, width, axis=dim), axis, backward)
        block = jnp.concatenate([low, block, high], axis=dim)
    return block


def swapped(block, axis, bit):
    count = lax.axis_size(axis)
    route = []
    for low in range(count):
        high = low | 1 << bit
        if high != low and high < count:
            route += [(low, high), (high, low)]
    return lax.ppermute(block, axis, route)


def lookup(table_row, type_ids):
    onehot = type_ids[None, :] == jnp.arange(table_row.shape[0], dtype=jnp.int32)[:, None]
    return jnp.sum(jnp.where(onehot, table_row[:, None], jnp.float32(0.0)), axis=0)


def pair_block(own_block, other_blocks, live_pairs, coupling_value):
    separation = own_block[0:3][None, :, :, None] - other_blocks[:, 0:3][:, :, None, :]
    radius_sq = jnp.sum(separation * separation, axis=1)
    sigma_pair = 0.5 * (own_block[3][None, :, None] + other_blocks[:, 3][:, None, :])
    depth_pair = jnp.sqrt(own_block[4][None, :, None] * other_blocks[:, 4][:, None, :])
    charges = own_block[5][None, :, None] * other_blocks[:, 5][:, None, :]
    flagged = jnp.maximum(own_block[6][None, :, None], other_blocks[:, 6][:, None, :])
    scaled = coupling_value * flagged
    sigma_two = sigma_pair * sigma_pair
    sigma_six = sigma_two * sigma_two * sigma_two
    soft_six = sigma_six * (soft_base + soft_alpha * scaled) + radius_sq * radius_sq * radius_sq
    soft_two = charge_base + charge_alpha * scaled + radius_sq
    inverse_six = 1.0 / soft_six
    energy_lj = (
        4.0
        * depth_pair
        * (sigma_six * sigma_six * inverse_six * inverse_six - sigma_six * inverse_six)
    )
    grad_six = (
        4.0
        * depth_pair
        * (
            sigma_six * inverse_six * inverse_six
            - 2.0 * sigma_six * sigma_six * inverse_six * inverse_six * inverse_six
        )
    )
    energy_coul = coulomb * charges * lax.rsqrt(soft_two)
    grad_two = -0.5 * energy_coul / soft_two
    weight = 1.0 - scaled
    total_pair = energy_lj + energy_coul
    pair_energy = jnp.sum(weight * total_pair * live_pairs)
    pair_dhdl = jnp.sum(
        flagged
        * (-total_pair + weight * (grad_six * sigma_six * soft_alpha + grad_two * charge_alpha))
        * live_pairs
    )
    force_scale = -weight * (6.0 * radius_sq * radius_sq * grad_six + 2.0 * grad_two) * live_pairs
    forces = jnp.sum(force_scale[:, None] * separation, axis=(0, 3))
    return (forces, pair_energy, pair_dhdl)


def block_terms(ghost_rows, listed_blocks, list_count, block_id, block_total, coupling_value):
    centre = 13 * block_total + block_id
    own_block = lax.dynamic_index_in_dim(ghost_rows, centre, 0, keepdims=False)
    other_blocks = jnp.take(ghost_rows, listed_blocks, axis=0)
    valid_slot = (jnp.arange(listed_blocks.shape[0], dtype=jnp.int32) < list_count).astype(
        jnp.float32
    )
    is_self = (listed_blocks == centre).astype(jnp.float32)[:, None, None] * jnp.eye(
        128, dtype=jnp.float32
    )[None]
    live_pairs = valid_slot[:, None, None] * (1.0 - is_self)
    return pair_block(own_block, other_blocks, live_pairs, coupling_value)


def on_device(
    fraction,
    atom_type,
    perturbed,
    leaving,
    neighbours,
    counts,
    sigma_table,
    depth_table,
    charge_table,
    domain_edge,
    coupling,
):
    atom_count = fraction.shape[-1]
    block_total = atom_count // 128
    spacing = float(atom_count) ** (1.0 / 3.0)
    type_ids = atom_type.reshape(atom_count)
    payload = jnp.concatenate(
        [
            fraction.reshape(3, atom_count),
            lookup(sigma_table, type_ids)[None],
            lookup(depth_table, type_ids)[None],
            lookup(charge_table, type_ids)[None],
            perturbed.reshape(1, atom_count).astype(jnp.float32),
        ],
        axis=0,
    )
    leave_slots = leaving.reshape(2, -1)
    shift_x = jnp.zeros((7, 1), jnp.float32).at[0].set(1.0)
    upward = payload[:, leave_slots[0]]
    downward = payload[:, leave_slots[1]]
    from_below = passed_along(upward, "dx", 1) - shift_x
    from_above = passed_along(downward, "dx", -1) + shift_x
    moved = payload.at[:, leave_slots[1]].set(from_below).at[:, leave_slots[0]].set(from_above)
    domain_block = moved.reshape(7, 1, 1, 1, atom_count)
    ghost_plane = extended(domain_block, (("dx", 1), ("dy", 2)), 1)
    partner = swapped(ghost_plane, "dz", 0)
    ghost_cells = jnp.concatenate([partner, ghost_plane, partner], axis=3)
    image_steps = jnp.arange(3, dtype=jnp.float32) - 1.0
    position = jnp.stack(
        [
            (ghost_cells[0] + image_steps[:, None, None, None]) * domain_edge[0] * spacing,
            (ghost_cells[1] + image_steps[None, :, None, None]) * domain_edge[1] * spacing,
            (ghost_cells[2] + image_steps[None, None, :, None]) * domain_edge[2] * spacing,
        ],
        axis=0,
    )
    ghost_all = jnp.concatenate([position, ghost_cells[3:]], axis=0)
    ghost_rows = (
        ghost_all.reshape(7, 27, block_total, 128)
        .transpose(1, 2, 0, 3)
        .reshape(27 * block_total, 7, 128)
    )
    listed = neighbours.reshape(block_total, -1)
    listed_count = counts.reshape(block_total)
    coupling_value = coupling[0]

    def one_block(block_id):
        return block_terms(
            ghost_rows,
            listed[block_id],
            listed_count[block_id],
            block_id,
            block_total,
            coupling_value,
        )

    forces, energies, dhdls = lax.map(one_block, jnp.arange(block_total, dtype=jnp.int32))
    forces = forces.transpose(1, 0, 2).reshape(3, 1, 1, 1, atom_count)
    window_energy, window_dhdl = lax.psum((jnp.sum(energies), jnp.sum(dhdls)), ("dx", "dy", "dz"))
    slot_total = jnp.float32(
        atom_count * lax.axis_size("dx") * lax.axis_size("dy") * lax.axis_size("dz")
    )
    energy = (0.5 * window_energy / slot_total).reshape(1)
    dhdl = (0.5 * window_dhdl / slot_total).reshape(1)
    return (forces, energy, dhdl)


def solution(mesh):
    return jax.shard_map(
        on_device,
        mesh=mesh,
        in_specs=(
            P(None, ("win", "dx"), "dy", "dz", None),
            P(("win", "dx"), "dy", "dz", None),
            P(("win", "dx"), "dy", "dz", None),
            P(("win", "dx"), "dy", "dz", None, None),
            P(("win", "dx"), "dy", "dz", None, None),
            P(("win", "dx"), "dy", "dz", None),
            P(),
            P(),
            P(),
            P(),
            P("win"),
        ),
        out_specs=(P(None, ("win", "dx"), "dy", "dz", None), P("win"), P("win")),
        check_vma=False,
    )
```

profile of v0, /device:TPU:0, one launch (start us, length us, event | category | flops | bytes accessed | tf_op | source)
XLA Modules:
  0.0 154.2 jit_solution(11909424343959024680)
XLA Ops:
  2.8 0.8 select_reduce_fusion
  5.1 3.1 %collective-permute-start = (f32[7,16]{0,1:T(8,128)S(1)}, f32[7,16]{0,1:T(8,128)S(1)}, u32[]{:S(2)}, u32[]{:S(2)}) collective-permute-start(f32[7,16]{0,1:T(8,128)S(1)} %bitcast.113), channel_id=1, source_target_pairs={{0,4},{4,8},{8,12},{12,0},{1,5},{5,9},{9,13},{13,1},{2,6},{6,10},{... | collective-permute-start | bytes 1352 | tf_op jit(solution)/shard_map/ppermute | solution.py:15
  8.8 2.1 %collective-permute-start.1 = (f32[7,16]{0,1:T(8,128)S(1)}, f32[7,16]{0,1:T(8,128)S(1)}, u32[]{:S(2)}, u32[]{:S(2)}) collective-permute-start(f32[7,16]{0,1:T(8,128)S(1)} %bitcast.112), channel_id=1, source_target_pairs={{0,12},{4,0},{8,4},{12,8},{1,13},{5,1},{9,5},{13,9},{2,14},{6,2},{... | collective-permute-start | bytes 1352 | tf_op jit(solution)/shard_map/ppermute | solution.py:15
  10.9 1.0 collective-permute-done
  11.9 0.9 scatter_custom_fusion
  12.9 0.8 scatter_custom_fusion.1
  13.7 3.5 %collective-permute-start.3 = (f32[7,1,1,1,768]{0,4,3,2,1:T(8,128)S(1)}, f32[7,1,1,1,768]{0,4,3,2,1:T(8,128)S(1)}, u32[]{:S(2)}, u32[]{:S(2)}) collective-permute-start(f32[7,1,1,1,768]{0,4,3,2,1:T(8,128)S(1)} %bitcast.97), channel_id=1, source_target_pairs={{4,0},{8,4},{12,8},{0,12},{5,1},{9,5},{13,9},{1,13},{6,2},{10,6},{... | collective-permute-start | bytes 64520 | tf_op jit(solution)/shard_map/ppermute | solution.py:27
  17.4 9.4 %collective-permute-done.3 = f32[7,1,1,1,768]{0,4,3,2,1:T(8,128)S(1)} collective-permute-done((f32[7,1,1,1,768]{0,4,3,2,1:T(8,128)S(1)}, f32[7,1,1,1,768]{0,4,3,2,1:T(8,128)S(1)}, u32[]{:S(2)}, u32[]{:S(2)}) %collective-permute-start.3) | collective-permute-done | bytes 21536 | tf_op jit(solution)/shard_map/ppermute | solution.py:27
  26.9 6.7 %collective-permute-done.2 = f32[7,1,1,1,768]{0,4,3,2,1:T(8,128)S(1)} collective-permute-done((f32[7,1,1,1,768]{0,4,3,2,1:T(8,128)S(1)}, f32[7,1,1,1,768]{0,4,3,2,1:T(8,128)S(1)}, u32[]{:S(2)}, u32[]{:S(2)}) %collective-permute-start.2) | collective-permute-done | bytes 21536 | tf_op jit(solution)/shard_map/ppermute | solution.py:24
  33.9 1.6 %collective-permute-start.5 = (f32[7,3,1,1,768]{4,3,2,1,0:T(1,128)S(1)}, f32[7,3,1,1,768]{4,3,2,1,0:T(1,128)S(1)}, u32[]{:S(2)}, u32[]{:S(2)}) collective-permute-start(f32[7,3,1,1,768]{4,3,2,1,0:T(1,128)S(1)} %pad_maximum_fusion.2), channel_id=1, source_target_pairs={{2,0},{0,2},{3,1},{1,3},{6,4},{4,6},{7,5},{5,7},{10,8},{8,10},{11,... | collective-permute-start | bytes 193544 | tf_op jit(solution)/shard_map/ppermute | solution.py:27
  36.0 2.2 %collective-permute-done.5 = f32[7,3,1,1,768]{4,3,2,1,0:T(1,128)S(1)} collective-permute-done((f32[7,3,1,1,768]{4,3,2,1,0:T(1,128)S(1)}, f32[7,3,1,1,768]{4,3,2,1,0:T(1,128)S(1)}, u32[]{:S(2)}, u32[]{:S(2)}) %collective-permute-start.5) | collective-permute-done | bytes 64544 | tf_op jit(solution)/shard_map/ppermute | solution.py:27
  38.2 1.5 collective-permute-done.4
  41.5 2.3 %fusion.34 = (f32[1,3,3,3,768]{4,0,3,2,1:T(1,128)S(1)}, f32[1,3,3,3,768]{4,0,3,2,1:T(1,128)S(1)}, f32[1,3,3,3,768]{4,0,3,2,1:T(1,128)S(1)}) fusion(f32[7,3,3,3,768]{4,0,3,2,1:T(8,128)S(1)} %copy_dynamic-update-slice_fusion.1, f32[3]{0:T(128)S(1)} %iota_add_fusion, f32[]{:T(128)} %bitcast.28, f32[]{:T(128)} %bitcast.32, f32[]{:T(128)} %bitcast.30), kind=kLoop, calls=%fused_computation.81 | loop fusion | flops 186624 | bytes 499212 | tf_op jit(solution)/shard_map/mul | solution.py:143
  44.2 72.7 %while.17 = (s32[]{:T(128)}, f32[6,3,128]{2,1,0:T(4,128)S(1)}, f32[6]{0:T(128)S(1)}, f32[6]{0:T(128)S(1)}, f32[]{:T(128)}, /*index=5*/s32[6]{0:T(128)S(1)}, f32[...) while((s32[]{:T(128)}, f32[6,3,128]{2,1,0:T(4,128)S(1)}, ...), condition=%wide.region_10.11_spmd, body=%wide.region_5.10_spmd.sunk | while | flops 20495192 | bytes 4781457 | solution.py:169
  50.5 3.8 %fusion.57 = (f32[]{:T(128)}, f32[]{:T(128)}, f32[16,128,128]{2,1,0:T(8,128)S(1)}) fusion(f32[128,128]{1,0:T(8,128)S(1)} %fusion.53, f32[16]{0:T(128)S(1)} %get-tuple-element.249, f32[16]{0:T(128)S(1)} %get-tuple-element.250, f32[16,128]{1,0:T(8,128)S(1)} %bitcast.104, f32[128]{0:T(128)S(1)} %get-tuple-element.253, f32[16,128]{1,0:T(8,128)S(1)} %bitcast.105, ...), kind=kLoop, calls=%fused_computation.33.clone.1 | loop fusion | flops 15990782 | bytes 2197644 | tf_op jit(solution)/shard_map/while/body/eval_jaxpr/reduce_sum | solution.py:78
  62.6 3.8 %fusion.57 = (f32[]{:T(128)}, f32[]{:T(128)}, f32[16,128,128]{2,1,0:T(8,128)S(1)}) fusion(f32[128,128]{1,0:T(8,128)S(1)} %fusion.53, f32[16]{0:T(128)S(1)} %get-tuple-element.249, f32[16]{0:T(128)S(1)} %get-tuple-element.250, f32[16,128]{1,0:T(8,128)S(1)} %bitcast.104, f32[128]{0:T(128)S(1)} %get-tuple-element.253, f32[16,128]{1,0:T(8,128)S(1)} %bitcast.105, ...), kind=kLoop, calls=%fused_computation.33.clone.1 | loop fusion | flops 15990782 | bytes 2197644 | tf_op jit(solution)/shard_map/while/body/eval_jaxpr/reduce_sum | solution.py:78
  66.9 0.8 dynamic_update_slice.25
  74.7 3.8 %fusion.57 = (f32[]{:T(128)}, f32[]{:T(128)}, f32[16,128,128]{2,1,0:T(8,128)S(1)}) fusion(f32[128,128]{1,0:T(8,128)S(1)} %fusion.53, f32[16]{0:T(128)S(1)} %get-tuple-element.249, f32[16]{0:T(128)S(1)} %get-tuple-element.250, f32[16,128]{1,0:T(8,128)S(1)} %bitcast.104, f32[128]{0:T(128)S(1)} %get-tuple-element.253, f32[16,128]{1,0:T(8,128)S(1)} %bitcast.105, ...), kind=kLoop, calls=%fused_computation.33.clone.1 | loop fusion | flops 15990782 | bytes 2197644 | tf_op jit(solution)/shard_map/while/body/eval_jaxpr/reduce_sum | solution.py:78
  86.8 3.8 %fusion.57 = (f32[]{:T(128)}, f32[]{:T(128)}, f32[16,128,128]{2,1,0:T(8,128)S(1)}) fusion(f32[128,128]{1,0:T(8,128)S(1)} %fusion.53, f32[16]{0:T(128)S(1)} %get-tuple-element.249, f32[16]{0:T(128)S(1)} %get-tuple-element.250, f32[16,128]{1,0:T(8,128)S(1)} %bitcast.104, f32[128]{0:T(128)S(1)} %get-tuple-element.253, f32[16,128]{1,0:T(8,128)S(1)} %bitcast.105, ...), kind=kLoop, calls=%fused_computation.33.clone.1 | loop fusion | flops 15990782 | bytes 2197644 | tf_op jit(solution)/shard_map/while/body/eval_jaxpr/reduce_sum | solution.py:78
  98.9 3.8 %fusion.57 = (f32[]{:T(128)}, f32[]{:T(128)}, f32[16,128,128]{2,1,0:T(8,128)S(1)}) fusion(f32[128,128]{1,0:T(8,128)S(1)} %fusion.53, f32[16]{0:T(128)S(1)} %get-tuple-element.249, f32[16]{0:T(128)S(1)} %get-tuple-element.250, f32[16,128]{1,0:T(8,128)S(1)} %bitcast.104, f32[128]{0:T(128)S(1)} %get-tuple-element.253, f32[16,128]{1,0:T(8,128)S(1)} %bitcast.105, ...), kind=kLoop, calls=%fused_computation.33.clone.1 | loop fusion | flops 15990782 | bytes 2197644 | tf_op jit(solution)/shard_map/while/body/eval_jaxpr/reduce_sum | solution.py:78
  103.2 0.8 dynamic_update_slice.25
  111.1 3.8 %fusion.57 = (f32[]{:T(128)}, f32[]{:T(128)}, f32[16,128,128]{2,1,0:T(8,128)S(1)}) fusion(f32[128,128]{1,0:T(8,128)S(1)} %fusion.53, f32[16]{0:T(128)S(1)} %get-tuple-element.249, f32[16]{0:T(128)S(1)} %get-tuple-element.250, f32[16,128]{1,0:T(8,128)S(1)} %bitcast.104, f32[128]{0:T(128)S(1)} %get-tuple-element.253, f32[16,128]{1,0:T(8,128)S(1)} %bitcast.105, ...), kind=kLoop, calls=%fused_computation.33.clone.1 | loop fusion | flops 15990782 | bytes 2197644 | tf_op jit(solution)/shard_map/while/body/eval_jaxpr/reduce_sum | solution.py:78
  115.4 0.8 dynamic_update_slice.25
  118.7 31.8 %all-reduce = (f32[]{:T(128)}, f32[]{:T(128)}) all-reduce(f32[]{:T(128)} %reduce_sum.96, f32[]{:T(128)} %reduce_sum.97), channel_id=1, replica_groups=mesh['win'=2,'dx'=4,'dy'=2,'dz'=2] {'dx','dy','dz'}, use_global_device_ids=true, to_apply=%region_12.13 | all-reduce | flops 2 | bytes 16 | tf_op jit(solution)/shard_map/psum | solution.py:171
  (151 shorter events, 36.6 us)
Async XLA Ops:
  0.6 12.2 %copy-start.2 = (f32[7]{0:T(128)S(1)}, f32[7]{0:T(128)}, u32[]{:S(2)}) copy-start(f32[7]{0:T(128)} %constant.159.clone.1) | copy-start | bytes 88
  5.1 6.8 %collective-permute-start = (f32[7,16]{0,1:T(8,128)S(1)}, f32[7,16]{0,1:T(8,128)S(1)}, u32[]{:S(2)}, u32[]{:S(2)}) collective-permute-start(f32[7,16]{0,1:T(8,128)S(1)} %bitcast.113), channel_id=1, source_target_pairs={{0,4},{4,8},{8,12},{12,0},{1,5},{5,9},{9,13},{13,1},{2,6},{6,10},{... | collective-permute-start | bytes 1352 | tf_op jit(solution)/shard_map/ppermute | solution.py:15
  8.8 27.1 %copy-start.1 = (s32[1,1,1,6,16]{4,2,3,1,0:T(1,128)S(1)}, s32[1,1,1,6,16]{4,2,3,1,0:T(1,128)}, u32[]{:S(2)}) copy-start(s32[1,1,1,6,16]{4,2,3,1,0:T(1,128)} %param.19) | copy-start | bytes 1156
  8.8 4.0 %collective-permute-start.1 = (f32[7,16]{0,1:T(8,128)S(1)}, f32[7,16]{0,1:T(8,128)S(1)}, u32[]{:S(2)}, u32[]{:S(2)}) collective-permute-start(f32[7,16]{0,1:T(8,128)S(1)} %bitcast.112), channel_id=1, source_target_pairs={{0,12},{4,0},{8,4},{12,8},{1,13},{5,1},{9,5},{13,9},{2,14},{6,2},{... | collective-permute-start | bytes 1352 | tf_op jit(solution)/shard_map/ppermute | solution.py:15
  12.8 27.1 %copy-start = (f32[3]{0:T(128)S(1)}, f32[3]{0:T(128)}, u32[]{:S(2)}) copy-start(f32[3]{0:T(128)} %param.24) | copy-start | bytes 40
  13.7 13.0 %collective-permute-start.3 = (f32[7,1,1,1,768]{0,4,3,2,1:T(8,128)S(1)}, f32[7,1,1,1,768]{0,4,3,2,1:T(8,128)S(1)}, u32[]{:S(2)}, u32[]{:S(2)}) collective-permute-start(f32[7,1,1,1,768]{0,4,3,2,1:T(8,128)S(1)} %bitcast.97), channel_id=1, source_target_pairs={{4,0},{8,4},{12,8},{0,12},{5,1},{9,5},{13,9},{1,13},{6,2},{10,6},{... | collective-permute-start | bytes 64520 | tf_op jit(solution)/shard_map/ppermute | solution.py:27
  17.2 16.4 %collective-permute-start.2 = (f32[7,1,1,1,768]{0,4,3,2,1:T(8,128)S(1)}, f32[7,1,1,1,768]{0,4,3,2,1:T(8,128)S(1)}, u32[]{:S(2)}, u32[]{:S(2)}) collective-permute-start(f32[7,1,1,1,768]{0,4,3,2,1:T(8,128)S(1)} %bitcast.98), channel_id=1, source_target_pairs={{0,4},{4,8},{8,12},{12,0},{1,5},{5,9},{9,13},{13,1},{2,6},{6,10},{... | collective-permute-start | bytes 64520 | tf_op jit(solution)/shard_map/ppermute | solution.py:24
  33.9 4.3 %collective-permute-start.5 = (f32[7,3,1,1,768]{4,3,2,1,0:T(1,128)S(1)}, f32[7,3,1,1,768]{4,3,2,1,0:T(1,128)S(1)}, u32[]{:S(2)}, u32[]{:S(2)}) collective-permute-start(f32[7,3,1,1,768]{4,3,2,1,0:T(1,128)S(1)} %pad_maximum_fusion.2), channel_id=1, source_target_pairs={{2,0},{0,2},{3,1},{1,3},{6,4},{4,6},{7,5},{5,7},{10,8},{8,10},{11,... | collective-permute-start | bytes 193544 | tf_op jit(solution)/shard_map/ppermute | solution.py:27
  35.4 4.3 %collective-permute-start.4 = (f32[7,3,1,1,768]{4,3,2,1,0:T(1,128)S(1)}, f32[7,3,1,1,768]{4,3,2,1,0:T(1,128)S(1)}, u32[]{:S(2)}, u32[]{:S(2)}) collective-permute-start(f32[7,3,1,1,768]{4,3,2,1,0:T(1,128)S(1)} %pad_maximum_fusion.2), channel_id=1, source_target_pairs={{0,2},{2,0},{1,3},{3,1},{4,6},{6,4},{5,7},{7,5},{8,10},{10,8},{9,1... | collective-permute-start | bytes 193544 | tf_op jit(solution)/shard_map/ppermute | solution.py:24
  39.8 1.5 collective-permute-start.6
  41.5 2.7 %copy-start.3 = (s32[1,1,1,6]{3,2,1,0:T(1,128)S(1)}, s32[1,1,1,6]{3,2,1,0:T(1,128)}, u32[]{:S(2)}) copy-start(s32[1,1,1,6]{3,2,1,0:T(1,128)} %param.20) | copy-start | bytes 76
where the time goes:
time: 155 us; the launch traced here: 154 us
  other arithmetic  41.6 us (27%)
  blocking collectives  31.8 us (21%)
  local copies, waits for them, and re-layouts  23.9 us (15%)
  waiting for transfers between devices  21.5 us (14%)
  loops' own time  20 us (13%)
  starting transfers between devices  10.9 us (7%)
  between operations  4.44 us (3%)
    psum x1, blocking collectives, on_device(): lax.psum((jnp.sum(energies), jnp.sum(dhdls)), ('dx', 'dy', 'dz'))  31.8 us
    reduce_sum x6, other arithmetic, pair_block(): jnp.sum(flagged * (-total_pair + weight * (grad_six * sigma_six * soft_al...  23.1 us
    another operation x1, loops' own time, on_device(): lax.map(one_block, jnp.arange(block_total, dtype=jnp.int32))  20 us
    ppermute x2, waiting for transfers between devices, extended(): lax.ppermute(lax.slice_in_dim(block, 0, width, axis=dim), axis, backward)  11.6 us
    dynamic_update_slice x18, local copies, waits for them, and re-layouts, on_device(): lax.map(one_block, jnp.arange(block_total, dtype=jnp.int32))  9.16 us
    ppermute x2, waiting for transfers between devices, extended(): lax.ppermute(lax.slice_in_dim(block, block.shape[dim] - width, None, axis...  8.23 us
    ppermute x2, starting transfers between devices, passed_along(): lax.ppermute(array, axis, [(i, (i + by) % devices) for i in range(devices)])  5.2 us
    ppermute x2, starting transfers between devices, extended(): lax.ppermute(lax.slice_in_dim(block, 0, width, axis=dim), axis, backward)  5.1 us
  transfers between devices with their start and end apart: 7, of which 6 were waited for; matrix products, arithmetic and copies ran while one was open for 2% of the time, Pallas kernels for 0%

commit v1 on v0

--- a/solution.py
+++ b/solution.py
@@ -8,6 +8,11 @@
 charge_base = 0.3
 charge_alpha = 0.5
 coulomb = 0.1
+
+
+def axis_by_axis(x, first, second):
+    inner = lax.psum(x, first)
+    return lax.psum(inner, second)
 
 
 def passed_along(array, axis, by):
@@ -168,7 +173,9 @@
 
     forces, energies, dhdls = lax.map(one_block, jnp.arange(block_total, dtype=jnp.int32))
     forces = forces.transpose(1, 0, 2).reshape(3, 1, 1, 1, atom_count)
-    window_energy, window_dhdl = lax.psum((jnp.sum(energies), jnp.sum(dhdls)), ("dx", "dy", "dz"))
+    window_energy, window_dhdl = axis_by_axis(
+        (jnp.sum(energies), jnp.sum(dhdls)), "dx", ("dy", "dz")
+    )
     slot_total = jnp.float32(
         atom_count * lax.axis_size("dx") * lax.axis_size("dy") * lax.axis_size("dz")
     )

time: 155 us -> 141 us (0.910)
  blocking collectives: 31.8 us -> 17.1 us
    psum x1 -> x2, blocking collectives: 31.8 us -> 17.1 us  [the longest x1 10.8 us: axis_by_axis(): inner = lax.psum(x, first)]
where the time goes in v1:
time: 141 us; the launch traced here: 139 us
  other arithmetic  41.6 us (30%)
  local copies, waits for them, and re-layouts  23.9 us (17%)
  waiting for transfers between devices  21.5 us (15%)
  loops' own time  20 us (14%)
  blocking collectives  17.1 us (12%)
  starting transfers between devices  10.9 us (8%)
  between operations  4.44 us (3%)
    reduce_sum x6, other arithmetic, pair_block(): jnp.sum(flagged * (-total_pair + weight * (grad_six * sigma_six * soft_al...  23.1 us
    another operation x1, loops' own time, on_device(): lax.map(one_block, jnp.arange(block_total, dtype=jnp.int32))  20 us
    ppermute x2, waiting for transfers between devices, extended(): lax.ppermute(lax.slice_in_dim(block, 0, width, axis=dim), axis, backward)  11.6 us
    psum x1, blocking collectives, axis_by_axis(): inner = lax.psum(x, first)  10.8 us
    dynamic_update_slice x18, local copies, waits for them, and re-layouts, on_device(): lax.map(one_block, jnp.arange(block_total, dtype=jnp.int32))  9.16 us
    ppermute x2, waiting for transfers between devices, extended(): lax.ppermute(lax.slice_in_dim(block, block.shape[dim] - width, None, axis...  8.23 us
    psum x1, blocking collectives, axis_by_axis(): return lax.psum(inner, second)  6.35 us
    ppermute x2, starting transfers between devices, passed_along(): lax.ppermute(array, axis, [(i, (i + by) % devices) for i in range(devices)])  5.2 us
  transfers between devices with their start and end apart: 7, of which 6 were waited for; matrix products, arithmetic and copies ran while one was open for 2% of the time, Pallas kernels for 0%

profile of v1, /device:TPU:0, one launch (start us, length us, event | category | flops | bytes accessed | tf_op | source)
XLA Modules:
  0.0 139.4 jit_solution(8250437965450649995)
XLA Ops:
  2.8 0.8 select_reduce_fusion
  5.1 3.1 %collective-permute-start = (f32[7,16]{0,1:T(8,128)S(1)}, f32[7,16]{0,1:T(8,128)S(1)}, u32[]{:S(2)}, u32[]{:S(2)}) collective-permute-start(f32[7,16]{0,1:T(8,128)S(1)} %bitcast.113), channel_id=1, source_target_pairs={{0,4},{4,8},{8,12},{12,0},{1,5},{5,9},{9,13},{13,1},{2,6},{6,10},{... | collective-permute-start | bytes 1352 | tf_op jit(solution)/shard_map/ppermute | solution.py:20
  8.8 2.1 %collective-permute-start.1 = (f32[7,16]{0,1:T(8,128)S(1)}, f32[7,16]{0,1:T(8,128)S(1)}, u32[]{:S(2)}, u32[]{:S(2)}) collective-permute-start(f32[7,16]{0,1:T(8,128)S(1)} %bitcast.112), channel_id=1, source_target_pairs={{0,12},{4,0},{8,4},{12,8},{1,13},{5,1},{9,5},{13,9},{2,14},{6,2},{... | collective-permute-start | bytes 1352 | tf_op jit(solution)/shard_map/ppermute | solution.py:20
  10.9 1.0 collective-permute-done
  11.9 0.9 scatter_custom_fusion
  12.9 0.8 scatter_custom_fusion.1
  13.7 3.5 %collective-permute-start.3 = (f32[7,1,1,1,768]{0,4,3,2,1:T(8,128)S(1)}, f32[7,1,1,1,768]{0,4,3,2,1:T(8,128)S(1)}, u32[]{:S(2)}, u32[]{:S(2)}) collective-permute-start(f32[7,1,1,1,768]{0,4,3,2,1:T(8,128)S(1)} %bitcast.97), channel_id=1, source_target_pairs={{4,0},{8,4},{12,8},{0,12},{5,1},{9,5},{13,9},{1,13},{6,2},{10,6},{... | collective-permute-start | bytes 64520 | tf_op jit(solution)/shard_map/ppermute | solution.py:32
  17.4 9.4 %collective-permute-done.3 = f32[7,1,1,1,768]{0,4,3,2,1:T(8,128)S(1)} collective-permute-done((f32[7,1,1,1,768]{0,4,3,2,1:T(8,128)S(1)}, f32[7,1,1,1,768]{0,4,3,2,1:T(8,128)S(1)}, u32[]{:S(2)}, u32[]{:S(2)}) %collective-permute-start.3) | collective-permute-done | bytes 21536 | tf_op jit(solution)/shard_map/ppermute | solution.py:32
  26.9 6.7 %collective-permute-done.2 = f32[7,1,1,1,768]{0,4,3,2,1:T(8,128)S(1)} collective-permute-done((f32[7,1,1,1,768]{0,4,3,2,1:T(8,128)S(1)}, f32[7,1,1,1,768]{0,4,3,2,1:T(8,128)S(1)}, u32[]{:S(2)}, u32[]{:S(2)}) %collective-permute-start.2) | collective-permute-done | bytes 21536 | tf_op jit(solution)/shard_map/ppermute | solution.py:29
  33.9 1.6 %collective-permute-start.5 = (f32[7,3,1,1,768]{4,3,2,1,0:T(1,128)S(1)}, f32[7,3,1,1,768]{4,3,2,1,0:T(1,128)S(1)}, u32[]{:S(2)}, u32[]{:S(2)}) collective-permute-start(f32[7,3,1,1,768]{4,3,2,1,0:T(1,128)S(1)} %pad_maximum_fusion.2), channel_id=1, source_target_pairs={{2,0},{0,2},{3,1},{1,3},{6,4},{4,6},{7,5},{5,7},{10,8},{8,10},{11,... | collective-permute-start | bytes 193544 | tf_op jit(solution)/shard_map/ppermute | solution.py:32
  36.0 2.2 %collective-permute-done.5 = f32[7,3,1,1,768]{4,3,2,1,0:T(1,128)S(1)} collective-permute-done((f32[7,3,1,1,768]{4,3,2,1,0:T(1,128)S(1)}, f32[7,3,1,1,768]{4,3,2,1,0:T(1,128)S(1)}, u32[]{:S(2)}, u32[]{:S(2)}) %collective-permute-start.5) | collective-permute-done | bytes 64544 | tf_op jit(solution)/shard_map/ppermute | solution.py:32
  38.2 1.5 %collective-permute-done.4 = f32[7,3,1,1,768]{4,3,2,1,0:T(1,128)S(1)} collective-permute-done((f32[7,3,1,1,768]{4,3,2,1,0:T(1,128)S(1)}, f32[7,3,1,1,768]{4,3,2,1,0:T(1,128)S(1)}, u32[]{:S(2)}, u32[]{:S(2)}) %collective-permute-start.4) | collective-permute-done | bytes 64544 | tf_op jit(solution)/shard_map/ppermute | solution.py:29
  41.5 2.3 %fusion.34 = (f32[1,3,3,3,768]{4,0,3,2,1:T(1,128)S(1)}, f32[1,3,3,3,768]{4,0,3,2,1:T(1,128)S(1)}, f32[1,3,3,3,768]{4,0,3,2,1:T(1,128)S(1)}) fusion(f32[7,3,3,3,768]{4,0,3,2,1:T(8,128)S(1)} %copy_dynamic-update-slice_fusion.1, f32[3]{0:T(128)S(1)} %iota_add_fusion, f32[]{:T(128)} %bitcast.28, f32[]{:T(128)} %bitcast.32, f32[]{:T(128)} %bitcast.30), kind=kLoop, calls=%fused_computation.81 | loop fusion | flops 186624 | bytes 499212 | tf_op jit(solution)/shard_map/mul | solution.py:148
  44.2 72.7 %while.17 = (s32[]{:T(128)}, f32[6,3,128]{2,1,0:T(4,128)S(1)}, f32[6]{0:T(128)S(1)}, f32[6]{0:T(128)S(1)}, f32[]{:T(128)}, /*index=5*/s32[6]{0:T(128)S(1)}, f32[...) while((s32[]{:T(128)}, f32[6,3,128]{2,1,0:T(4,128)S(1)}, ...), condition=%wide.region_10.11_spmd, body=%wide.region_5.10_spmd.sunk | while | flops 20495192 | bytes 4781457 | solution.py:174
  50.5 3.8 %fusion.57 = (f32[]{:T(128)}, f32[]{:T(128)}, f32[16,128,128]{2,1,0:T(8,128)S(1)}) fusion(f32[128,128]{1,0:T(8,128)S(1)} %fusion.53, f32[16]{0:T(128)S(1)} %get-tuple-element.251, f32[16]{0:T(128)S(1)} %get-tuple-element.252, f32[16,128]{1,0:T(8,128)S(1)} %bitcast.104, f32[128]{0:T(128)S(1)} %get-tuple-element.255, f32[16,128]{1,0:T(8,128)S(1)} %bitcast.105, ...), kind=kLoop, calls=%fused_computation.33.clone.1 | loop fusion | flops 15990782 | bytes 2197644 | tf_op jit(solution)/shard_map/while/body/eval_jaxpr/reduce_sum | solution.py:83
  62.6 3.8 %fusion.57 = (f32[]{:T(128)}, f32[]{:T(128)}, f32[16,128,128]{2,1,0:T(8,128)S(1)}) fusion(f32[128,128]{1,0:T(8,128)S(1)} %fusion.53, f32[16]{0:T(128)S(1)} %get-tuple-element.251, f32[16]{0:T(128)S(1)} %get-tuple-element.252, f32[16,128]{1,0:T(8,128)S(1)} %bitcast.104, f32[128]{0:T(128)S(1)} %get-tuple-element.255, f32[16,128]{1,0:T(8,128)S(1)} %bitcast.105, ...), kind=kLoop, calls=%fused_computation.33.clone.1 | loop fusion | flops 15990782 | bytes 2197644 | tf_op jit(solution)/shard_map/while/body/eval_jaxpr/reduce_sum | solution.py:83
  66.9 0.8 dynamic_update_slice.25
  74.7 3.8 %fusion.57 = (f32[]{:T(128)}, f32[]{:T(128)}, f32[16,128,128]{2,1,0:T(8,128)S(1)}) fusion(f32[128,128]{1,0:T(8,128)S(1)} %fusion.53, f32[16]{0:T(128)S(1)} %get-tuple-element.251, f32[16]{0:T(128)S(1)} %get-tuple-element.252, f32[16,128]{1,0:T(8,128)S(1)} %bitcast.104, f32[128]{0:T(128)S(1)} %get-tuple-element.255, f32[16,128]{1,0:T(8,128)S(1)} %bitcast.105, ...), kind=kLoop, calls=%fused_computation.33.clone.1 | loop fusion | flops 15990782 | bytes 2197644 | tf_op jit(solution)/shard_map/while/body/eval_jaxpr/reduce_sum | solution.py:83
  86.8 3.8 %fusion.57 = (f32[]{:T(128)}, f32[]{:T(128)}, f32[16,128,128]{2,1,0:T(8,128)S(1)}) fusion(f32[128,128]{1,0:T(8,128)S(1)} %fusion.53, f32[16]{0:T(128)S(1)} %get-tuple-element.251, f32[16]{0:T(128)S(1)} %get-tuple-element.252, f32[16,128]{1,0:T(8,128)S(1)} %bitcast.104, f32[128]{0:T(128)S(1)} %get-tuple-element.255, f32[16,128]{1,0:T(8,128)S(1)} %bitcast.105, ...), kind=kLoop, calls=%fused_computation.33.clone.1 | loop fusion | flops 15990782 | bytes 2197644 | tf_op jit(solution)/shard_map/while/body/eval_jaxpr/reduce_sum | solution.py:83
  98.9 3.8 %fusion.57 = (f32[]{:T(128)}, f32[]{:T(128)}, f32[16,128,128]{2,1,0:T(8,128)S(1)}) fusion(f32[128,128]{1,0:T(8,128)S(1)} %fusion.53, f32[16]{0:T(128)S(1)} %get-tuple-element.251, f32[16]{0:T(128)S(1)} %get-tuple-element.252, f32[16,128]{1,0:T(8,128)S(1)} %bitcast.104, f32[128]{0:T(128)S(1)} %get-tuple-element.255, f32[16,128]{1,0:T(8,128)S(1)} %bitcast.105, ...), kind=kLoop, calls=%fused_computation.33.clone.1 | loop fusion | flops 15990782 | bytes 2197644 | tf_op jit(solution)/shard_map/while/body/eval_jaxpr/reduce_sum | solution.py:83
  103.2 0.8 dynamic_update_slice.25
  111.1 3.8 %fusion.57 = (f32[]{:T(128)}, f32[]{:T(128)}, f32[16,128,128]{2,1,0:T(8,128)S(1)}) fusion(f32[128,128]{1,0:T(8,128)S(1)} %fusion.53, f32[16]{0:T(128)S(1)} %get-tuple-element.251, f32[16]{0:T(128)S(1)} %get-tuple-element.252, f32[16,128]{1,0:T(8,128)S(1)} %bitcast.104, f32[128]{0:T(128)S(1)} %get-tuple-element.255, f32[16,128]{1,0:T(8,128)S(1)} %bitcast.105, ...), kind=kLoop, calls=%fused_computation.33.clone.1 | loop fusion | flops 15990782 | bytes 2197644 | tf_op jit(solution)/shard_map/while/body/eval_jaxpr/reduce_sum | solution.py:83
  118.7 10.8 %all-reduce.1 = (f32[]{:T(128)}, f32[]{:T(128)}) all-reduce(f32[]{:T(128)} %reduce_sum.96, f32[]{:T(128)} %reduce_sum.97), channel_id=1, replica_groups=mesh['win'=2,'dx'=4,'dy'=2,'dz'=2] {'dx'}, use_global_device_ids=true, to_apply=%region_12.13 | all-reduce | flops 2 | bytes 16 | tf_op jit(solution)/shard_map/psum | solution.py:14
  129.5 6.3 %all-reduce = (f32[]{:T(128)}, f32[]{:T(128)}) all-reduce(f32[]{:T(128)} %get-tuple-element.158, f32[]{:T(128)} %get-tuple-element.159), channel_id=1, replica_groups=mesh['win'=2,'dx'=4,'dy'=2,'dz'=2] {'dy','dz'}, use_global_device_ids=true, to_apply=%region_13.14 | all-reduce | flops 2 | bytes 16 | tf_op jit(solution)/shard_map/psum | solution.py:15
  (152 shorter events, 37.3 us)
Async XLA Ops:
  0.6 12.2 %copy-start.2 = (f32[7]{0:T(128)S(1)}, f32[7]{0:T(128)}, u32[]{:S(2)}) copy-start(f32[7]{0:T(128)} %constant.159.clone.1) | copy-start | bytes 88
  5.1 6.8 %collective-permute-start = (f32[7,16]{0,1:T(8,128)S(1)}, f32[7,16]{0,1:T(8,128)S(1)}, u32[]{:S(2)}, u32[]{:S(2)}) collective-permute-start(f32[7,16]{0,1:T(8,128)S(1)} %bitcast.113), channel_id=1, source_target_pairs={{0,4},{4,8},{8,12},{12,0},{1,5},{5,9},{9,13},{13,1},{2,6},{6,10},{... | collective-permute-start | bytes 1352 | tf_op jit(solution)/shard_map/ppermute | solution.py:20
  8.8 27.1 %copy-start.1 = (s32[1,1,1,6,16]{4,2,3,1,0:T(1,128)S(1)}, s32[1,1,1,6,16]{4,2,3,1,0:T(1,128)}, u32[]{:S(2)}) copy-start(s32[1,1,1,6,16]{4,2,3,1,0:T(1,128)} %param.19) | copy-start | bytes 1156
  8.8 4.0 %collective-permute-start.1 = (f32[7,16]{0,1:T(8,128)S(1)}, f32[7,16]{0,1:T(8,128)S(1)}, u32[]{:S(2)}, u32[]{:S(2)}) collective-permute-start(f32[7,16]{0,1:T(8,128)S(1)} %bitcast.112), channel_id=1, source_target_pairs={{0,12},{4,0},{8,4},{12,8},{1,13},{5,1},{9,5},{13,9},{2,14},{6,2},{... | collective-permute-start | bytes 1352 | tf_op jit(solution)/shard_map/ppermute | solution.py:20
  12.8 27.1 %copy-start = (f32[3]{0:T(128)S(1)}, f32[3]{0:T(128)}, u32[]{:S(2)}) copy-start(f32[3]{0:T(128)} %param.24) | copy-start | bytes 40
  13.7 13.0 %collective-permute-start.3 = (f32[7,1,1,1,768]{0,4,3,2,1:T(8,128)S(1)}, f32[7,1,1,1,768]{0,4,3,2,1:T(8,128)S(1)}, u32[]{:S(2)}, u32[]{:S(2)}) collective-permute-start(f32[7,1,1,1,768]{0,4,3,2,1:T(8,128)S(1)} %bitcast.97), channel_id=1, source_target_pairs={{4,0},{8,4},{12,8},{0,12},{5,1},{9,5},{13,9},{1,13},{6,2},{10,6},{... | collective-permute-start | bytes 64520 | tf_op jit(solution)/shard_map/ppermute | solution.py:32
  17.2 16.4 %collective-permute-start.2 = (f32[7,1,1,1,768]{0,4,3,2,1:T(8,128)S(1)}, f32[7,1,1,1,768]{0,4,3,2,1:T(8,128)S(1)}, u32[]{:S(2)}, u32[]{:S(2)}) collective-permute-start(f32[7,1,1,1,768]{0,4,3,2,1:T(8,128)S(1)} %bitcast.98), channel_id=1, source_target_pairs={{0,4},{4,8},{8,12},{12,0},{1,5},{5,9},{9,13},{13,1},{2,6},{6,10},{... | collective-permute-start | bytes 64520 | tf_op jit(solution)/shard_map/ppermute | solution.py:29
  33.9 4.3 %collective-permute-start.5 = (f32[7,3,1,1,768]{4,3,2,1,0:T(1,128)S(1)}, f32[7,3,1,1,768]{4,3,2,1,0:T(1,128)S(1)}, u32[]{:S(2)}, u32[]{:S(2)}) collective-permute-start(f32[7,3,1,1,768]{4,3,2,1,0:T(1,128)S(1)} %pad_maximum_fusion.2), channel_id=1, source_target_pairs={{2,0},{0,2},{3,1},{1,3},{6,4},{4,6},{7,5},{5,7},{10,8},{8,10},{11,... | collective-permute-start | bytes 193544 | tf_op jit(solution)/shard_map/ppermute | solution.py:32
  35.4 4.3 %collective-permute-start.4 = (f32[7,3,1,1,768]{4,3,2,1,0:T(1,128)S(1)}, f32[7,3,1,1,768]{4,3,2,1,0:T(1,128)S(1)}, u32[]{:S(2)}, u32[]{:S(2)}) collective-permute-start(f32[7,3,1,1,768]{4,3,2,1,0:T(1,128)S(1)} %pad_maximum_fusion.2), channel_id=1, source_target_pairs={{0,2},{2,0},{1,3},{3,1},{4,6},{6,4},{5,7},{7,5},{8,10},{10,8},{9,1... | collective-permute-start | bytes 193544 | tf_op jit(solution)/shard_map/ppermute | solution.py:29
  39.8 1.5 %collective-permute-start.6 = (f32[7,3,3,1,768]{4,3,2,1,0:T(1,128)S(1)}, f32[7,3,3,1,768]{4,3,2,1,0:T(1,128)S(1)}, u32[]{:S(2)}, u32[]{:S(2)}) collective-permute-start(f32[7,3,3,1,768]{4,3,2,1,0:T(1,128)S(1)} %pad_maximum_fusion.1), channel_id=1, source_target_pairs={{0,1},{1,0},{2,3},{3,2},{4,5},{5,4},{6,7},{7,6},{8,9},{9,8},{10,11... | collective-permute-start | bytes 580616 | tf_op jit(solution)/shard_map/ppermute | solution.py:44
  41.5 2.7 %copy-start.3 = (s32[1,1,1,6]{3,2,1,0:T(1,128)S(1)}, s32[1,1,1,6]{3,2,1,0:T(1,128)}, u32[]{:S(2)}) copy-start(s32[1,1,1,6]{3,2,1,0:T(1,128)} %param.20) | copy-start | bytes 76
